TPU v7x, 32 devices: a whole 2x2x4 slice. The times are simulated.
32 devices in a mesh: obs: 4 (over z), face: 8 (over y, x, core).
Axes of the slice: x: 2, y: 2, z: 4, core: 2. Of those that a mesh axis runs over, the one named last changes fastest.
Arguments:
- density: float32 [34, 8192], P(None, ('obs', 'face')), may hold values from 0.6 to 1.4
- velocity: float32 [3, 34, 8192], P(None, None, ('obs', 'face')), may hold values from -6 to 6
- pressure: float32 [34, 8192], P(None, ('obs', 'face')), may hold values from -6 to 6
- normal: float32 [3, 8192], P(None, ('obs', 'face')), may hold values from -1 to 1, as said below
- direction: float32 [32, 8, 3], P(('obs', 'face')), may hold values from -1 to 1, as said below
- weights: bfloat16 [32, 8, 768, 256], P(('obs', 'face')), may hold values from -0.21875 to 0.21875
- bin_index: int32 [32, 8], P(('obs', 'face')), may hold values from 0 to 7, as said below
- group_index: int32 [32, 8], P(('obs', 'face')), may hold values from 0 to 3
- item_count: int32 [32], P(('obs', 'face')), may hold values from 4 to 8, as said below
Outputs:
- signal: float32 [256, 1024], P('face', 'obs')
Inputs may be any that keep to these rules, and one draw needn't show every extreme that they name: `bin_index`: no time block is named more than 2 times in one device's list; in every draw some device names a block 2 times among its live entries. `item_count`: some device has all 8 entries live. Each face's normal has unit length. Each entry's direction has unit length.
All inputs are finite; a program needn't handle non-finite values.
Results may differ from a plain program's by a relative error of at most 0.0029.
Values sent between devices are 32-bit elements; how exact they have to be, the bound alone decides.
A program may use at most 64 MiB of HBM per device.

v0:
```python
import functools

import jax
import jax.numpy as jnp
from jax import lax
from jax.experimental import pallas as pl
from jax.experimental.pallas import tpu as pltpu
from jax.sharding import PartitionSpec as P

SLOT_CAP = 2
MESH = pl.DeviceIdType.MESH


def loop(first, last, body):
    if last - first <= 8:
        for at in range(first, last):
            body(at)
    else:
        lax.fori_loop(first, last, lambda at, _: (body(at), _)[1], 0)


def kernel(
    n_obs, n_face, chunks,
    direction, bin_index, group_index, item_count,
    density, velocity, pressure, normal, weights,
    out,
    dens, veloc, press, norms, matrices, thick, rate_of, load_of, sources, blocks,
    outgoing, arrived, labels_out, labels_in, grouped, owned,
    in_sem, weight_sem, label_send, label_recv, send_sem, recv_sem, send_two, recv_two,
):
    my_obs, my_face = lax.axis_index("obs"), lax.axis_index("face")
    list_total = matrices.shape[1]
    steps, width = thick.shape
    part = width // chunks

    loads = [
        pltpu.make_async_copy(density, dens, in_sem.at[0]),
        pltpu.make_async_copy(velocity, veloc, in_sem.at[1]),
        pltpu.make_async_copy(pressure, press, in_sem.at[2]),
        pltpu.make_async_copy(normal, norms, in_sem.at[3]),
    ]
    for copy in loads:
        copy.start()

    def weight_copy(chunk, listed):
        return pltpu.make_async_copy(
            weights.at[0, listed, :, pl.ds(chunk * part, part)],
            matrices.at[chunk, listed],
            weight_sem.at[chunk, listed],
        )

    for chunk in range(chunks):
        loop(0, list_total, lambda listed: weight_copy(chunk, listed).start())

    barrier = pltpu.get_barrier_semaphore()

    def greet_face(shift):
        peer = lax.rem(my_face + shift, n_face)
        pl.semaphore_signal(barrier, inc=1, device_id=(my_obs, peer), device_id_type=MESH)

    def greet_obs(shift):
        peer = lax.rem(my_obs + shift, n_obs)
        pl.semaphore_signal(barrier, inc=1, device_id=(peer, my_face), device_id_type=MESH)

    loop(1, n_face, greet_face)
    loop(1, n_obs, greet_obs)

    live_count = item_count[0]

    def slots_of(block):
        last = jnp.int32(-1)
        first = jnp.int32(-1)
        for listed in range(list_total):
            match = (bin_index[0, listed] == block) & (listed < live_count)
            last = jnp.where(match, listed, last)
        for listed in reversed(range(list_total)):
            match = (bin_index[0, listed] == block) & (listed < live_count)
            first = jnp.where(match, listed, first)
        return first, last

    upper = lax.broadcasted_iota(jnp.int32, labels_out.shape[1:], 0) < 4

    def fill_labels(block):
        first, last = slots_of(block)
        label_first = group_index[0, jnp.maximum(first, 0)]
        label_last = group_index[0, jnp.maximum(last, 0)]
        return jnp.where(upper, label_first, label_last)

    def label_copy(shift):
        peer = lax.rem(my_face + shift, n_face)
        return pltpu.make_async_remote_copy(
            src_ref=labels_out.at[peer],
            dst_ref=labels_in.at[my_face],
            send_sem=label_send.at[shift - 1],
            recv_sem=label_recv.at[shift - 1],
            device_id=(my_obs, peer),
            device_id_type=MESH,
        )

    def set_label(shift):
        peer = lax.rem(my_face + shift, n_face)
        labels_out[peer] = fill_labels(peer)

    loop(1, n_face, set_label)

    for copy in loads:
        copy.wait()
    n0, n1, n2 = norms[0:1], norms[1:2], norms[2:3]
    v0, v1, v2 = veloc[0], veloc[1], veloc[2]
    density_now, pressure_now = dens[...], press[...]
    normal_speed = v0 * n0 + v1 * n1 + v2 * n2
    flux = density_now * normal_speed
    thick[...] = (0.5 * (flux[2:] - flux[:-2])).astype(jnp.bfloat16)
    for c, (n, v) in enumerate(((n0, v0), (n1, v1), (n2, v2))):
        load = pressure_now * n + density_now * v * normal_speed
        rate_of[c] = 0.5 * (load[2:] - load[:-2])
        load_of[c] = load[1:-1]

    def prepare(listed):
        h0, h1, h2 = (direction[c, 0, listed] for c in range(3))
        rate = h0 * rate_of[0] + h1 * rate_of[1] + h2 * rate_of[2]
        radial = h0 * load_of[0] + h1 * load_of[1] + h2 * load_of[2]
        sources[listed] = jnp.concatenate(
            [thick[...], rate.astype(jnp.bfloat16), radial.astype(jnp.bfloat16)], axis=1
        )

    loop(0, list_total, prepare)
    pl.semaphore_wait(barrier, n_face + n_obs - 2)
    loop(1, n_face, lambda shift: label_copy(shift).start())

    batch = 8 if list_total % 8 == 0 else 1

    def compute(chunk, at):
        members = [at * batch + offset for offset in range(batch)]
        for listed in members:
            weight_copy(chunk, listed).wait()
        products = [
            jnp.dot(sources[listed], matrices[chunk, listed], preferred_element_type=jnp.float32)
            for listed in members
        ]
        for listed, product in zip(members, products):
            blocks[chunk, listed] = product

    def data_copy(chunk, shift):
        peer = lax.rem(my_face + shift, n_face)
        return pltpu.make_async_remote_copy(
            src_ref=outgoing.at[chunk, peer],
            dst_ref=arrived.at[chunk, my_face],
            send_sem=send_sem.at[chunk, shift - 1],
            recv_sem=recv_sem.at[chunk, shift - 1],
            device_id=(my_obs, peer),
            device_id_type=MESH,
        )

    def route(chunk, block):
        first, last = slots_of(block)
        early = blocks[chunk, jnp.maximum(first, 0)]
        late = blocks[chunk, jnp.maximum(last, 0)]
        return jnp.where(last >= 0, early, 0.0), jnp.where(last > first, late, 0.0)

    for chunk in range(chunks):
        loop(0, list_total // batch, functools.partial(compute, chunk))

        def send(shift):
            peer = lax.rem(my_face + shift, n_face)
            early, late = route(chunk, peer)
            outgoing[chunk, peer, :steps] = early
            outgoing[chunk, peer, steps:] = late
            data_copy(chunk, shift).start()

        loop(1, n_face, send)

    def selected(early, late, label_first, label_last):
        return [
            jnp.where(label_first == group, early, 0.0) + jnp.where(label_last == group, late, 0.0)
            for group in range(n_obs)
        ]

    def obs_copy(chunk, shift):
        peer = lax.rem(my_obs + shift, n_obs)
        return pltpu.make_async_remote_copy(
            src_ref=grouped.at[chunk, peer],
            dst_ref=owned.at[chunk, my_obs],
            send_sem=send_two.at[chunk, shift - 1],
            recv_sem=recv_two.at[chunk, shift - 1],
            device_id=(peer, my_face),
            device_id_type=MESH,
        )

    own_labels = fill_labels(my_face)
    for chunk in range(chunks):
        early, late = route(chunk, my_face)
        sums = tuple(selected(early, late, own_labels[0:1], own_labels[4:5]))

        def collect(shift, sums, chunk=chunk):
            source = lax.rem(my_face + n_face - shift, n_face)
            if chunk == 0:
                label_copy(shift).wait_recv()
            data_copy(chunk, shift).wait_recv()
            labels = labels_in[source]
            both = arrived[chunk, source]
            terms = selected(both[:steps], both[steps:], labels[0:1], labels[4:5])
            return tuple(a + b for a, b in zip(sums, terms))

        if n_face <= 8:
            for shift in range(1, n_face):
                sums = collect(shift, sums)
        else:
            sums = lax.fori_loop(1, n_face, collect, sums)
        for group in range(n_obs):
            grouped[chunk, group] = sums[group]
        loop(1, n_obs, lambda shift: obs_copy(chunk, shift).start())

    for chunk in range(chunks):
        total = grouped[chunk, my_obs]
        for shift in range(1, n_obs):
            source = lax.rem(my_obs + n_obs - shift, n_obs)
            obs_copy(chunk, shift).wait_recv()
            total = total + owned[chunk, source]
        out[:, chunk * part:(chunk + 1) * part] = total

    for chunk in range(chunks):
        loop(1, n_face, lambda shift: data_copy(chunk, shift).wait_send())
        loop(1, n_obs, lambda shift: obs_copy(chunk, shift).wait_send())
    loop(1, n_face, lambda shift: label_copy(shift).wait_send())


def local(
    density, velocity, pressure, normal, direction, weights, bin_index, group_index, item_count
):
    n_face, n_obs = lax.axis_size("face"), lax.axis_size("obs")
    list_total, depth, width = weights.shape[1:]
    rows, faces = density.shape
    steps = rows - 2
    chunks = max(1, width // 128)
    part = width // chunks
    smem = pl.BlockSpec(memory_space=pltpu.SMEM)
    anywhere = pl.BlockSpec(memory_space=pl.ANY)
    f32 = jnp.float32
    return pl.pallas_call(
        functools.partial(kernel, n_obs, n_face, chunks),
        out_shape=pltpu.VMEM((steps, width), f32),
        in_specs=[smem] * 4 + [anywhere] * 5,
        out_specs=pl.BlockSpec(memory_space=pltpu.VMEM),
        scratch_shapes=[
            pltpu.VMEM((rows, faces), f32),
            pltpu.VMEM((3, rows, faces), f32),
            pltpu.VMEM((rows, faces), f32),
            pltpu.VMEM((3, faces), f32),
            pltpu.VMEM((chunks, list_total, depth, part), jnp.bfloat16),
            pltpu.VMEM((steps, faces), jnp.bfloat16),
            pltpu.VMEM((3, steps, faces), f32),
            pltpu.VMEM((3, steps, faces), f32),
            pltpu.VMEM((list_total, steps, depth), jnp.bfloat16),
            pltpu.VMEM((chunks, list_total, steps, part), f32),
            pltpu.VMEM((chunks, n_face, SLOT_CAP * steps, part), f32),
            pltpu.VMEM((chunks, n_face, SLOT_CAP * steps, part), f32),
            pltpu.VMEM((n_face, 8, part), jnp.int32),
            pltpu.VMEM((n_face, 8, part), jnp.int32),
            pltpu.VMEM((chunks, n_obs, steps, part), f32),
            pltpu.VMEM((chunks, n_obs, steps, part), f32),
            pltpu.SemaphoreType.DMA((4,)),
            pltpu.SemaphoreType.DMA((chunks, list_total)),
            pltpu.SemaphoreType.DMA((n_face - 1,)),
            pltpu.SemaphoreType.DMA((n_face - 1,)),
            pltpu.SemaphoreType.DMA((chunks, n_face - 1)),
            pltpu.SemaphoreType.DMA((chunks, n_face - 1)),
            pltpu.SemaphoreType.DMA((chunks, n_obs - 1)),
            pltpu.SemaphoreType.DMA((chunks, n_obs - 1)),
        ],
        compiler_params=pltpu.CompilerParams(
            collective_id=0, has_side_effects=True
        ),
    )(
        jnp.transpose(direction, (2, 0, 1)), bin_index, group_index, item_count,
        density, velocity, pressure, normal, weights,
    )


def solution(mesh):
    placed = (
        P(None, ("obs", "face")),
        P(None, None, ("obs", "face")),
        P(None, ("obs", "face")),
        P(None, ("obs", "face")),
        P(("obs", "face"), None, None),
        P(("obs", "face"), None, None, None),
        P(("obs", "face"), None),
        P(("obs", "face"), None),
        P(("obs", "face")),
    )
    return jax.shard_map(
        local, mesh=mesh, in_specs=placed, out_specs=P("face", "obs"), check_vma=False
    )
```

profile of v0, /device:TPU:0, one launch (start us, length us, event | category | flops | bytes accessed | tf_op | source)
XLA Modules:
  0.0 19.6 jit_solution(10382385682609894398)
XLA Ops:
  0.7 18.4 %shard_map.91 = f32[32,256]{1,0:T(8,128)S(1)} custom-call(f32[3,1,8]{2,1,0:T(1,128)} %bitcast.1, s32[1,8]{1,0:T(1,128)} %bin_index.1, s32[1,8]{1,0:T(1,128)} %group_index.1, s32[1]{0:T(128)S(6)} %copy.12.item_count, f32[34,256]{1,0:T(8,128)} %density.1, f32[3,34,256]{2,1,0:T(8,128)} %velocity.1, f32[34,256]{1,0:T(8,128)} %pressure.1, f32[3,256]{1,0:T(4,128)} %normal.1, ...), custom_call_target="tpu_custom_call" | custom-call | tf_op jit(solution)/shard_map/pallas_call | solution.py:240
  19.0 0.6 %copy.11 = f32[32,256]{1,0:T(8,128)} copy(f32[32,256]{1,0:T(8,128)S(1)} %shard_map.91) | data formatting | bytes 65536
where the time goes:
time: 19.8 us; the launch traced here: 19.6 us
  Pallas kernels  18.4 us (93%)
  between operations  0.66 us (3%)
  local copies, waits for them, and re-layouts  0.62 us (3%)
    pallas_call x1, Pallas kernels, local(): pl.pallas_call(functools.partial(kernel, n_obs, n_face, chunks), out_shap...  18.4 us
    unnamed x1, local copies, waits for them, and re-layouts  0.62 us

commit v1 on v0

v1 whole, which is shorter than its diff:
```python
import functools

import jax
import jax.numpy as jnp
from jax import lax
from jax.experimental import pallas as pl
from jax.experimental.pallas import tpu as pltpu
from jax.sharding import PartitionSpec as P

MESH = pl.DeviceIdType.MESH
PLANES = 2


def loop(first, last, body):
    if last - first <= 8:
        for at in range(first, last):
            body(at)
    else:
        lax.fori_loop(first, last, lambda at, _: (body(at), _)[1], 0)


def kernel(
    n_obs, n_face, planes, cores, chunks,
    direction_in, bin_in, group_in, item_count,
    density, velocity, pressure, normal, weights,
    out,
    direction, bin_index, group_index,
    dens, veloc, press, norms, matrices, thick, rate_of, load_of, sources,
    products, labels_out, labels_in, arrived, cells, owned,
    small_sem, in_sem, weight_sem, ready, label_send, label_recv,
    send_sem, recv_sem, send_two, recv_two,
):
    my_obs, my_face = lax.axis_index("obs"), lax.axis_index("face")
    listed_total, steps = sources.shape[:2]
    part = matrices.shape[3]
    groups = n_obs // planes
    members = planes * n_face
    owners_plane = n_face // cores
    owners = planes * owners_plane
    rows = steps // owners
    total_cells = n_obs * n_face
    lanes = min(128, members * listed_total)
    per_row = lanes // listed_total
    key_blocks = members // per_row

    my_group, my_plane = my_obs // planes, lax.rem(my_obs, planes)
    me = my_plane * n_face + my_face
    my_owner = my_plane * owners_plane + my_face // cores
    is_owner = lax.rem(my_face, cores) == cores - 1
    my_cell = my_obs * n_face + my_face

    def member_device(member):
        return (my_group * planes + member // n_face, lax.rem(member, n_face))

    def owner_device(owner):
        return (
            my_group * planes + owner // owners_plane,
            lax.rem(owner, owners_plane) * cores + cores - 1,
        )

    def counterpart(shift):
        return (lax.rem(my_obs + shift * planes, n_obs), my_face)

    smalls = [
        pltpu.make_async_copy(direction_in, direction, small_sem.at[0]),
        pltpu.make_async_copy(bin_in, bin_index, small_sem.at[1]),
        pltpu.make_async_copy(group_in, group_index, small_sem.at[2]),
    ]
    loads = [
        pltpu.make_async_copy(density, dens, in_sem.at[0]),
        pltpu.make_async_copy(velocity, veloc, in_sem.at[1]),
        pltpu.make_async_copy(pressure, press, in_sem.at[2]),
        pltpu.make_async_copy(normal, norms, in_sem.at[3]),
    ]
    for copy in smalls + loads:
        copy.start()

    def weight_copy(chunk, listed):
        return pltpu.make_async_copy(
            weights.at[0, listed, :, pl.ds(chunk * part, part)],
            matrices.at[chunk, listed],
            weight_sem.at[chunk, listed],
        )

    for chunk in range(chunks):
        loop(0, listed_total, lambda listed: weight_copy(chunk, listed).start())

    barrier = pltpu.get_barrier_semaphore()

    def greet(device):
        pl.semaphore_signal(barrier, inc=1, device_id=device, device_id_type=MESH)

    @pl.when(is_owner)
    def _():
        loop(1, members, lambda shift: greet(member_device(lax.rem(me + shift, members))))
        loop(1, groups, lambda shift: greet(counterpart(shift)))

    @pl.when(jnp.logical_not(is_owner))
    def _():
        loop(0, owners, lambda owner: greet(owner_device(owner)))

    for copy in smalls:
        copy.wait()
    live_count = item_count[0]
    lane = lax.broadcasted_iota(jnp.int32, (1, 128), 1) - lax.rem(me, per_row) * listed_total
    row = jnp.zeros((1, 128), jnp.int32)
    for listed in range(listed_total):
        label = group_index[0, listed] * n_face + bin_index[0, listed] + 1
        label = jnp.where(listed < live_count, label, 0)
        row = jnp.where(lane == listed, label, row)
    labels_out[...] = row

    for copy in loads:
        copy.wait()
    n0, n1, n2 = norms[0:1], norms[1:2], norms[2:3]
    v0, v1, v2 = veloc[0], veloc[1], veloc[2]
    density_now, pressure_now = dens[...], press[...]
    normal_speed = v0 * n0 + v1 * n1 + v2 * n2
    flux = density_now * normal_speed
    thick[...] = (0.5 * (flux[2:] - flux[:-2])).astype(jnp.bfloat16)
    for c, (n, v) in enumerate(((n0, v0), (n1, v1), (n2, v2))):
        load = pressure_now * n + density_now * v * normal_speed
        rate_of[c] = 0.5 * (load[2:] - load[:-2])
        load_of[c] = load[1:-1]

    def prepare(listed):
        h0, h1, h2 = (direction[c, 0, listed] for c in range(3))
        rate = h0 * rate_of[0] + h1 * rate_of[1] + h2 * rate_of[2]
        radial = h0 * load_of[0] + h1 * load_of[1] + h2 * load_of[2]
        sources[listed] = jnp.concatenate(
            [thick[...], rate.astype(jnp.bfloat16), radial.astype(jnp.bfloat16)], axis=1
        )

    loop(0, listed_total, prepare)

    def compute(chunk):
        for listed in range(listed_total):
            weight_copy(chunk, listed).wait()
            product = jnp.dot(
                sources[listed], matrices[chunk, listed], preferred_element_type=jnp.float32
            )
            products[chunk, pl.ds(listed, steps, stride=listed_total), :] = product

    def label_copy(owner):
        return pltpu.make_async_remote_copy(
            src_ref=labels_out,
            dst_ref=labels_in.at[me],
            send_sem=label_send,
            recv_sem=label_recv,
            device_id=owner_device(owner),
            device_id_type=MESH,
        )

    def rows_of(owner):
        size = rows * listed_total
        return pl.ds(pl.multiple_of(owner * size, size), size)

    def data_copy(chunk, owner):
        return pltpu.make_async_remote_copy(
            src_ref=products.at[chunk, rows_of(owner)],
            dst_ref=arrived.at[chunk, me],
            send_sem=send_sem.at[chunk],
            recv_sem=recv_sem.at[chunk],
            device_id=owner_device(owner),
            device_id_type=MESH,
        )

    def send_all(copy_of):
        @pl.when(is_owner)
        def _():
            loop(1, owners, lambda shift: copy_of(lax.rem(my_owner + shift, owners)).start())

        @pl.when(jnp.logical_not(is_owner))
        def _():
            loop(0, owners, lambda shift: copy_of(lax.rem(my_owner + shift, owners)).start())

    compute(0)
    pl.semaphore_wait(barrier, jnp.where(is_owner, members + groups - 2, owners))

    @pl.when(is_owner)
    def _():
        for shift in range(1, groups):
            pl.semaphore_signal(
                ready, inc=1, device_id=counterpart(shift), device_id_type=MESH
            )

    send_all(label_copy)
    send_all(functools.partial(data_copy, 0))
    for chunk in range(1, chunks):
        compute(chunk)
        send_all(functools.partial(data_copy, chunk))

    def wait_bytes(ref, sem):
        pltpu.make_async_copy(ref, ref, sem).wait()

    def cell_copy(chunk, cell):
        return pltpu.make_async_remote_copy(
            src_ref=cells.at[chunk, cell],
            dst_ref=owned.at[chunk, my_group * owners + my_owner],
            send_sem=send_two.at[chunk],
            recv_sem=recv_two.at[chunk],
            device_id=(cell // n_face, lax.rem(cell, n_face)),
            device_id_type=MESH,
        )

    @pl.when(is_owner)
    def _():
        labels_in[me] = labels_out[...]
        for chunk in range(chunks):
            arrived[chunk, me] = products[chunk, rows_of(my_owner)]
        wait_bytes(labels_in.at[pl.ds(0, members - 1)], label_recv)
        cell_number = lax.broadcasted_iota(jnp.int32, (total_cells, lanes), 0) + 1
        choose = []
        for block in range(key_blocks):
            keys = jnp.sum(labels_in[block * per_row:(block + 1) * per_row], axis=0)
            choose.append((keys[:, :lanes] == cell_number).astype(jnp.bfloat16))
        choose = jnp.concatenate(choose + choose, axis=1)
        for chunk in range(chunks):
            wait_bytes(arrived.at[chunk, pl.ds(0, members - 1)], recv_sem.at[chunk])
            values = jnp.concatenate(
                [
                    arrived[chunk, :, at * listed_total:(at + 1) * listed_total, :].reshape(
                        members * listed_total, part
                    )
                    for at in range(rows)
                ],
                axis=1,
            )
            high = values.astype(jnp.bfloat16)
            low = (values - high.astype(jnp.float32)).astype(jnp.bfloat16)
            sums = jnp.dot(
                choose,
                jnp.concatenate([high, low], axis=0),
                preferred_element_type=jnp.float32,
            )
            for at in range(rows):
                cells[chunk, :, at, :] = sums[:, at * part:(at + 1) * part]
            if chunk == 0 and groups > 1:
                pl.semaphore_wait(ready, groups - 1)
            loop(
                0,
                total_cells - 1,
                lambda at: cell_copy(chunk, at + (at >= my_cell).astype(jnp.int32)).start(),
            )
            owned[chunk, my_group * owners + my_owner] = cells[chunk, my_cell]

    senders = groups * owners
    for chunk in range(chunks):
        @pl.when(is_owner)
        def _():
            wait_bytes(owned.at[chunk, pl.ds(0, senders - 1)], recv_two.at[chunk])

        @pl.when(jnp.logical_not(is_owner))
        def _():
            wait_bytes(owned.at[chunk, pl.ds(0, senders)], recv_two.at[chunk])

        for owner in range(owners):
            total = owned[chunk, owner]
            for group in range(1, groups):
                total = total + owned[chunk, group * owners + owner]
            out[owner * rows:(owner + 1) * rows, chunk * part:(chunk + 1) * part] = total

    def drain(count):
        wait_bytes(labels_in.at[pl.ds(0, count)], label_send)
        for chunk in range(chunks):
            wait_bytes(arrived.at[chunk, pl.ds(0, count)], send_sem.at[chunk])

    @pl.when(is_owner)
    def _():
        drain(owners - 1)
        for chunk in range(chunks):
            wait_bytes(cells.at[chunk, pl.ds(0, total_cells - 1)], send_two.at[chunk])

    @pl.when(jnp.logical_not(is_owner))
    def _():
        drain(owners)


def local(
    density, velocity, pressure, normal, direction, weights, bin_index, group_index, item_count
):
    n_face, n_obs = lax.axis_size("face"), lax.axis_size("obs")
    listed_total, depth, width = weights.shape[1:]
    rows, faces = density.shape
    steps = rows - 2
    chunks = max(1, width // 128)
    part = width // chunks
    planes = PLANES if n_obs % PLANES == 0 else 1
    cores = 2 if n_face % 2 == 0 else 1
    members = planes * n_face
    owners = members // cores
    groups = n_obs // planes
    total_cells = n_obs * n_face
    own_rows = steps // owners
    smem = pl.BlockSpec(memory_space=pltpu.SMEM)
    anywhere = pl.BlockSpec(memory_space=pl.ANY)
    f32, i32 = jnp.float32, jnp.int32
    dma = pltpu.SemaphoreType.DMA
    return pl.pallas_call(
        functools.partial(kernel, n_obs, n_face, planes, cores, chunks),
        out_shape=pltpu.VMEM((steps, width), f32),
        in_specs=[anywhere] * 3 + [smem] + [anywhere] * 5,
        out_specs=pl.BlockSpec(memory_space=pltpu.VMEM),
        scratch_shapes=[
            pltpu.SMEM((3, 1, listed_total), f32),
            pltpu.SMEM((1, listed_total), i32),
            pltpu.SMEM((1, listed_total), i32),
            pltpu.VMEM((rows, faces), f32),
            pltpu.VMEM((3, rows, faces), f32),
            pltpu.VMEM((rows, faces), f32),
            pltpu.VMEM((3, faces), f32),
            pltpu.VMEM((chunks, listed_total, depth, part), jnp.bfloat16),
            pltpu.VMEM((steps, faces), jnp.bfloat16),
            pltpu.VMEM((3, steps, faces), f32),
            pltpu.VMEM((3, steps, faces), f32),
            pltpu.VMEM((listed_total, steps, depth), jnp.bfloat16),
            pltpu.VMEM((chunks, steps * listed_total, part), f32),
            pltpu.VMEM((1, 128), i32),
            pltpu.VMEM((members, 1, 128), i32),
            pltpu.VMEM((chunks, members, own_rows * listed_total, part), f32),
            pltpu.VMEM((chunks, total_cells, own_rows, part), f32),
            pltpu.VMEM((chunks, groups * owners, own_rows, part), f32),
            dma((3,)),
            dma((4,)),
            dma((chunks, listed_total)),
            pltpu.SemaphoreType.REGULAR,
            dma,
            dma,
            dma((chunks,)),
            dma((chunks,)),
            dma((chunks,)),
            dma((chunks,)),
        ],
        compiler_params=pltpu.CompilerParams(
            collective_id=0, has_side_effects=True
        ),
    )(
        jnp.transpose(direction, (2, 0, 1)), bin_index, group_index, item_count,
        density, velocity, pressure, normal, weights,
    )


def solution(mesh):
    placed = (
        P(None, ("obs", "face")),
        P(None, None, ("obs", "face")),
        P(None, ("obs", "face")),
        P(None, ("obs", "face")),
        P(("obs", "face"), None, None),
        P(("obs", "face"), None, None, None),
        P(("obs", "face"), None),
        P(("obs", "face"), None),
        P(("obs", "face")),
    )
    return jax.shard_map(
        local, mesh=mesh, in_specs=placed, out_specs=P("face", "obs"), check_vma=False
    )
```

time: 19.8 us -> 17.7 us (0.89)
  Pallas kernels: 18.4 us -> 16.3 us
    pallas_call x1, Pallas kernels: 18.4 us -> 16.3 us  [local(): pl.pallas_call(functools.partial(kernel, n_obs, n_face, planes, cores, ch...]
where the time goes in v1:
time: 17.7 us; the launch traced here: 17.6 us
  Pallas kernels  16.3 us (92%)
  between operations  0.66 us (4%)
  local copies, waits for them, and re-layouts  0.62 us (4%)
    pallas_call x1, Pallas kernels, local(): pl.pallas_call(functools.partial(kernel, n_obs, n_face, planes, cores, ch...  16.3 us
    unnamed x1, local copies, waits for them, and re-layouts  0.62 us

profile of v1, /device:TPU:0, one launch (start us, length us, event | category | flops | bytes accessed | tf_op | source)
XLA Modules:
  0.0 17.6 jit_solution(3361113998788006686)
XLA Ops:
  0.7 16.3 %shard_map.91 = f32[32,256]{1,0:T(8,128)S(1)} custom-call(f32[3,1,8]{2,1,0:T(1,128)} %bitcast.1, s32[1,8]{1,0:T(1,128)} %bin_in.1, s32[1,8]{1,0:T(1,128)} %group_in.1, s32[1]{0:T(128)S(6)} %copy.12.item_count, f32[34,256]{1,0:T(8,128)} %density.1, f32[3,34,256]{2,1,0:T(8,128)} %velocity.1, f32[34,256]{1,0:T(8,128)} %pressure.1, f32[3,256]{1,0:T(4,128)} %normal.1, ...), custom_call_target="tpu_custom_call" | custom-call | tf_op jit(solution)/shard_map/pallas_call | solution.py:299
  17.0 0.6 %copy.11 = f32[32,256]{1,0:T(8,128)} copy(f32[32,256]{1,0:T(8,128)S(1)} %shard_map.91) | data formatting | bytes 65536

commit v2 on v1

--- a/solution.py
+++ b/solution.py
@@ -8,7 +8,8 @@
 from jax.sharding import PartitionSpec as P
 
 MESH = pl.DeviceIdType.MESH
-PLANES = 2
+BATCH = 8
+PLANES = 1
 
 
 def loop(first, last, body):
@@ -134,12 +135,18 @@
     loop(0, listed_total, prepare)
 
     def compute(chunk):
-        for listed in range(listed_total):
-            weight_copy(chunk, listed).wait()
-            product = jnp.dot(
-                sources[listed], matrices[chunk, listed], preferred_element_type=jnp.float32
-            )
-            products[chunk, pl.ds(listed, steps, stride=listed_total), :] = product
+        for first in range(0, listed_total, BATCH):
+            batch = range(first, min(first + BATCH, listed_total))
+            for listed in batch:
+                weight_copy(chunk, listed).wait()
+            results = [
+                jnp.dot(
+                    sources[listed], matrices[chunk, listed], preferred_element_type=jnp.float32
+                )
+                for listed in batch
+            ]
+            for listed, product in zip(batch, results):
+                products[chunk, pl.ds(listed, steps, stride=listed_total), :] = product
 
     def label_copy(owner):
         return pltpu.make_async_remote_copy(

time: 17.7 us -> 16.6 us (0.938)
  Pallas kernels: 16.3 us -> 15.1 us
    pallas_call x1, Pallas kernels: 16.3 us -> 15.1 us  [local(): pl.pallas_call(functools.partial(kernel, n_obs, n_face, planes, cores, ch...]
where the time goes in v2:
time: 16.6 us; the launch traced here: 16.4 us
  Pallas kernels  15.1 us (91%)
  between operations  0.66 us (4%)
  local copies, waits for them, and re-layouts  0.62 us (4%)
    pallas_call x1, Pallas kernels, local(): pl.pallas_call(functools.partial(kernel, n_obs, n_face, planes, cores, ch...  15.1 us
    unnamed x1, local copies, waits for them, and re-layouts  0.62 us

profile of v2, /device:TPU:0, one launch (start us, length us, event | category | flops | bytes accessed | tf_op | source)
XLA Modules:
  0.0 16.4 jit_solution(3478344900078968717)
XLA Ops:
  0.7 15.1 %shard_map.91 = f32[32,256]{1,0:T(8,128)S(1)} custom-call(f32[3,1,8]{2,1,0:T(1,128)} %bitcast.1, s32[1,8]{1,0:T(1,128)} %bin_in.1, s32[1,8]{1,0:T(1,128)} %group_in.1, s32[1]{0:T(128)S(6)} %copy.12.item_count, f32[34,256]{1,0:T(8,128)} %density.1, f32[3,34,256]{2,1,0:T(8,128)} %velocity.1, f32[34,256]{1,0:T(8,128)} %pressure.1, f32[3,256]{1,0:T(4,128)} %normal.1, ...), custom_call_target="tpu_custom_call" | custom-call | tf_op jit(solution)/shard_map/pallas_call | solution.py:306
  15.8 0.6 %copy.11 = f32[32,256]{1,0:T(8,128)} copy(f32[32,256]{1,0:T(8,128)S(1)} %shard_map.91) | data formatting | bytes 65536

commit v3 on v2

v3 whole, which is shorter than its diff:
```python
import functools

import jax
import jax.numpy as jnp
from jax import lax
from jax.experimental import pallas as pl
from jax.experimental.pallas import tpu as pltpu
from jax.sharding import PartitionSpec as P

MESH = pl.DeviceIdType.MESH
BATCH = 8
SLOT_CAP = 2
EARLY = 2
PLANES = 1


def loop(first, last, body):
    if last - first <= 8:
        for at in range(first, last):
            body(at)
    else:
        lax.fori_loop(first, last, lambda at, _: (body(at), _)[1], 0)


def kernel(
    n_obs, n_face, planes, cores, chunks, early,
    direction_in, bin_in, group_in, item_count,
    density, velocity, pressure, normal, weights,
    out,
    direction, bin_index, group_index,
    dens, veloc, press, norms, matrices, thick, rate_of, load_of, sources,
    products, labels_out, labels_in, arrived, partial, first_cells, cells, owned,
    small_sem, in_sem, weight_sem, entered, ready, label_send, label_recv,
    send_sem, recv_sem, send_two, recv_two,
):
    my_obs, my_face = lax.axis_index("obs"), lax.axis_index("face")
    listed_total, steps = sources.shape[:2]
    part = matrices[0].shape[2]
    groups = n_obs // planes
    members = planes * n_face
    owners_plane = n_face // cores
    owners = planes * owners_plane
    rows = steps // owners
    total_cells = n_obs * n_face
    waves, half = products.shape[1], listed_total // products.shape[1]
    fold = max(1, 8 // half)
    tile = fold * half
    tiles = rows // fold
    lanes = min(128, members * tile)
    per_row = lanes // tile
    key_blocks = members // per_row

    my_group, my_plane = my_obs // planes, lax.rem(my_obs, planes)
    me = my_plane * n_face + my_face
    my_owner = my_plane * owners_plane + my_face // cores
    is_owner = lax.rem(my_face, cores) == cores - 1
    my_cell = my_obs * n_face + my_face

    def member_device(member):
        return (my_group * planes + member // n_face, lax.rem(member, n_face))

    def owner_device(owner, core=cores - 1):
        return (
            my_group * planes + owner // owners_plane,
            lax.rem(owner, owners_plane) * cores + core,
        )

    def counterpart(shift):
        return (lax.rem(my_obs + shift * planes, n_obs), my_face)

    smalls = [
        pltpu.make_async_copy(direction_in, direction, small_sem.at[0]),
        pltpu.make_async_copy(bin_in, bin_index, small_sem.at[1]),
        pltpu.make_async_copy(group_in, group_index, small_sem.at[2]),
    ]
    loads = [
        pltpu.make_async_copy(density, dens, in_sem.at[0]),
        pltpu.make_async_copy(velocity, veloc, in_sem.at[1]),
        pltpu.make_async_copy(pressure, press, in_sem.at[2]),
        pltpu.make_async_copy(normal, norms, in_sem.at[3]),
    ]
    for copy in smalls + loads:
        copy.start()

    def weight_copy(chunk, listed):
        return pltpu.make_async_copy(
            weights.at[0, listed, :, pl.ds(chunk * part, part)],
            matrices[chunk].at[listed],
            weight_sem.at[chunk, listed],
        )

    loop(0, listed_total, lambda listed: weight_copy(0, listed).start())

    barrier = pltpu.get_barrier_semaphore()

    def tell(semaphore, device):
        pl.semaphore_signal(semaphore, inc=1, device_id=device, device_id_type=MESH)

    def greet(device):
        tell(barrier, device)

    @pl.when(is_owner)
    def _():
        loop(1, owners, lambda shift: greet(owner_device(lax.rem(my_owner + shift, owners))))
        loop(1, groups, lambda shift: greet(counterpart(shift)))
        for core in range(cores - 1):
            loop(0, owners, lambda owner: greet(owner_device(owner, core)))

    for chunk in range(1, chunks):
        loop(0, listed_total, lambda listed: weight_copy(chunk, listed).start())
    for copy in smalls:
        copy.wait()
    live_count = item_count[0]
    urgent, label_of = [], []
    for listed in range(listed_total):
        label = group_index[0, listed] * n_face + bin_index[0, listed]
        live = listed < live_count
        urgent.append((live & (label < early)).astype(jnp.int32))
    urgent_total = sum(urgent)
    picked = [jnp.int32(0) for _ in range(listed_total)]
    ahead = jnp.int32(0)
    for listed in range(listed_total):
        place = jnp.where(urgent[listed] == 1, ahead, urgent_total + listed - ahead)
        ahead = ahead + urgent[listed]
        picked = [jnp.where(place == at, listed, old) for at, old in enumerate(picked)]

    lane = lax.broadcasted_iota(jnp.int32, (1, 128), 1) - lax.rem(me, per_row) * tile
    for wave in range(waves):
        row = jnp.zeros((1, 128), jnp.int32)
        for at in range(half):
            listed = picked[wave * half + at]
            label = group_index[0, listed] * n_face + bin_index[0, listed] + 1
            label = jnp.where(listed < live_count, label, 0)
            for copy_at in range(fold):
                row = jnp.where(lane == copy_at * half + at, label, row)
        labels_out[wave] = row

    for copy in loads:
        copy.wait()
    n0, n1, n2 = norms[0:1], norms[1:2], norms[2:3]
    v0, v1, v2 = veloc[0], veloc[1], veloc[2]
    density_now, pressure_now = dens[...], press[...]
    normal_speed = v0 * n0 + v1 * n1 + v2 * n2
    flux = density_now * normal_speed
    thick[...] = (0.5 * (flux[2:] - flux[:-2])).astype(jnp.bfloat16)
    for c, (n, v) in enumerate(((n0, v0), (n1, v1), (n2, v2))):
        load = pressure_now * n + density_now * v * normal_speed
        rate_of[c] = 0.5 * (load[2:] - load[:-2])
        load_of[c] = load[1:-1]

    def prepare(slot):
        h0, h1, h2 = (direction[c, 0, picked[slot]] for c in range(3))
        rate = h0 * rate_of[0] + h1 * rate_of[1] + h2 * rate_of[2]
        radial = h0 * load_of[0] + h1 * load_of[1] + h2 * load_of[2]
        sources[slot] = jnp.concatenate(
            [thick[...], rate.astype(jnp.bfloat16), radial.astype(jnp.bfloat16)], axis=1
        )

    for slot in range(listed_total):
        prepare(slot)

    def compute(chunk):
        for listed in range(listed_total):
            weight_copy(chunk, listed).wait()
        for first in range(0, listed_total, BATCH):
            batch = range(first, min(first + BATCH, listed_total))
            results = [
                jnp.dot(
                    sources[slot],
                    matrices[chunk][picked[slot]],
                    preferred_element_type=jnp.float32,
                )
                for slot in batch
            ]
            for slot, product in zip(batch, results):
                wave, at = divmod(slot, half)
                products[chunk, wave, pl.ds(at, steps, stride=half), :] = product

    def label_copy(owner):
        return pltpu.make_async_remote_copy(
            src_ref=labels_out,
            dst_ref=labels_in.at[me],
            send_sem=label_send,
            recv_sem=label_recv,
            device_id=owner_device(owner),
            device_id_type=MESH,
        )

    def rows_of(owner):
        size = rows * half
        return pl.ds(pl.multiple_of(owner * size, size), size)

    def data_copy(chunk, wave, owner):
        return pltpu.make_async_remote_copy(
            src_ref=products.at[chunk, wave, rows_of(owner)],
            dst_ref=arrived.at[chunk, wave, me],
            send_sem=send_sem.at[chunk, wave],
            recv_sem=recv_sem.at[chunk, wave],
            device_id=owner_device(owner),
            device_id_type=MESH,
        )

    def send_all(copy_of):
        @pl.when(is_owner)
        def _():
            loop(1, owners, lambda shift: copy_of(lax.rem(my_owner + shift, owners)).start())

        @pl.when(jnp.logical_not(is_owner))
        def _():
            loop(0, owners, lambda shift: copy_of(lax.rem(my_owner + shift, owners)).start())

    compute(0)
    pl.semaphore_wait(barrier, jnp.where(is_owner, owners + groups - 2, owners))

    @pl.when(jnp.logical_not(is_owner))
    def _():
        loop(0, owners, lambda owner: tell(entered, owner_device(owner)))

    send_all(label_copy)
    send_all(functools.partial(data_copy, 0, 0))
    for chunk in range(1, chunks):
        compute(chunk)
        send_all(functools.partial(data_copy, chunk, 0))
    for wave in range(1, waves):
        for chunk in range(chunks):
            send_all(functools.partial(data_copy, chunk, wave))

    def wait_bytes(ref, sem):
        pltpu.make_async_copy(ref, ref, sem).wait()

    def cell_copy(source, chunk, cell):
        return pltpu.make_async_remote_copy(
            src_ref=source.at[chunk, cell],
            dst_ref=owned.at[chunk, my_group * owners + my_owner],
            send_sem=send_two.at[chunk],
            recv_sem=recv_two.at[chunk],
            device_id=(cell // n_face, cell % n_face),
            device_id_type=MESH,
        )

    def send_cells(source, chunk, first, last):
        def send(cell):
            @pl.when(cell != my_cell)
            def _():
                cell_copy(source, chunk, cell).start()

        for cell in range(first, last):
            send(cell)

        @pl.when((my_cell >= first) & (my_cell < last))
        def _():
            owned[chunk, my_group * owners + my_owner] = source[chunk, my_cell]

    @pl.when(is_owner)
    def _():
        if cores > 1:
            pl.semaphore_wait(entered, members - owners)
        for shift in range(1, groups):
            tell(ready, counterpart(shift))
        labels_in[me] = labels_out[...]
        for chunk in range(chunks):
            for wave in range(waves):
                arrived[chunk, wave, me] = products[chunk, wave, rows_of(my_owner)]
        wait_bytes(labels_in.at[pl.ds(0, members - 1)], label_recv)
        shape = (fold * total_cells, lanes)
        line = lax.broadcasted_iota(jnp.int32, shape, 0)
        place = lax.rem(lax.broadcasted_iota(jnp.int32, shape, 1), tile) // half
        chosen = []
        for wave in range(waves):
            parts = []
            for block in range(key_blocks):
                keys = jnp.sum(labels_in[block * per_row:(block + 1) * per_row, wave], axis=0)
                match = keys[:, :lanes] + place * total_cells == line + 1
                live = keys[:, :lanes] > 0
                parts.append((match & live).astype(jnp.float32).astype(jnp.bfloat16))
            chosen.append(jnp.concatenate(parts + parts, axis=1))

        for wave in range(waves):
            for chunk in range(chunks):
                wait_bytes(
                    arrived.at[chunk, wave, pl.ds(0, members - 1)], recv_sem.at[chunk, wave]
                )
                values = jnp.concatenate(
                    [
                        arrived[chunk, wave, :, at * tile:(at + 1) * tile, :].reshape(
                            members * tile, part
                        )
                        for at in range(tiles)
                    ],
                    axis=1,
                )
                high = values.astype(jnp.bfloat16)
                low = (values - high.astype(jnp.float32)).astype(jnp.bfloat16)
                sums = jnp.dot(
                    chosen[wave],
                    jnp.concatenate([high, low], axis=0),
                    preferred_element_type=jnp.float32,
                )
                if wave > 0:
                    sums = sums + partial[chunk]
                if wave < waves - 1:
                    partial[chunk] = sums
                count = total_cells if wave == waves - 1 else early
                target = cells if wave == waves - 1 else first_cells
                if wave in (0, waves - 1):
                    for at in range(rows):
                        tile_at, line_at = divmod(at, fold)
                        target[chunk, :, at, :] = sums[
                            line_at * total_cells:line_at * total_cells + count,
                            tile_at * part:(tile_at + 1) * part,
                        ]
                if wave == 0 and chunk == 0 and groups > 1:
                    pl.semaphore_wait(ready, groups - 1)
                if waves > 1 and wave == 0:
                    send_cells(first_cells, chunk, 0, early)
                if wave == waves - 1:
                    send_cells(cells, chunk, early if waves > 1 else 0, total_cells)

    senders = groups * owners
    for chunk in range(chunks):
        @pl.when(is_owner)
        def _():
            wait_bytes(owned.at[chunk, pl.ds(0, senders - 1)], recv_two.at[chunk])

        @pl.when(jnp.logical_not(is_owner))
        def _():
            wait_bytes(owned.at[chunk, pl.ds(0, senders)], recv_two.at[chunk])

        for owner in range(owners):
            total = owned[chunk, owner]
            for group in range(1, groups):
                total = total + owned[chunk, group * owners + owner]
            out[owner * rows:(owner + 1) * rows, chunk * part:(chunk + 1) * part] = total

    def drain(count):
        wait_bytes(labels_in.at[pl.ds(0, count)], label_send)
        for chunk in range(chunks):
            for wave in range(waves):
                wait_bytes(arrived.at[chunk, wave, pl.ds(0, count)], send_sem.at[chunk, wave])

    @pl.when(is_owner)
    def _():
        drain(owners - 1)
        for chunk in range(chunks):
            wait_bytes(cells.at[chunk, pl.ds(0, total_cells - 1)], send_two.at[chunk])

    @pl.when(jnp.logical_not(is_owner))
    def _():
        drain(owners)


def local(
    density, velocity, pressure, normal, direction, weights, bin_index, group_index, item_count
):
    n_face, n_obs = lax.axis_size("face"), lax.axis_size("obs")
    listed_total, depth, width = weights.shape[1:]
    rows, faces = density.shape
    steps = rows - 2
    chunks = max(1, width // 128)
    part = width // chunks
    planes = PLANES if n_obs % PLANES == 0 else 1
    cores = 2 if n_face % 2 == 0 else 1
    members = planes * n_face
    owners = members // cores
    groups = n_obs // planes
    total_cells = n_obs * n_face
    own_rows = steps // owners
    waves = 2 if listed_total % 2 == 0 and own_rows % max(1, 16 // listed_total) == 0 else 1
    half = listed_total // waves
    fold = max(1, 8 // half)
    early = min(EARLY, half // SLOT_CAP, n_face)
    smem = pl.BlockSpec(memory_space=pltpu.SMEM)
    anywhere = pl.BlockSpec(memory_space=pl.ANY)
    f32, i32 = jnp.float32, jnp.int32
    dma = pltpu.SemaphoreType.DMA
    return pl.pallas_call(
        functools.partial(kernel, n_obs, n_face, planes, cores, chunks, early),
        out_shape=pltpu.VMEM((steps, width), f32),
        in_specs=[anywhere] * 3 + [smem] + [anywhere] * 5,
        out_specs=pl.BlockSpec(memory_space=pltpu.VMEM),
        scratch_shapes=[
            pltpu.SMEM((3, 1, listed_total), f32),
            pltpu.SMEM((1, listed_total), i32),
            pltpu.SMEM((1, listed_total), i32),
            pltpu.VMEM((rows, faces), f32),
            pltpu.VMEM((3, rows, faces), f32),
            pltpu.VMEM((rows, faces), f32),
            pltpu.VMEM((3, faces), f32),
            [pltpu.VMEM((listed_total, depth, part), jnp.bfloat16)] * chunks,
            pltpu.VMEM((steps, faces), jnp.bfloat16),
            pltpu.VMEM((3, steps, faces), f32),
            pltpu.VMEM((3, steps, faces), f32),
            pltpu.VMEM((listed_total, steps, depth), jnp.bfloat16),
            pltpu.VMEM((chunks, waves, steps * half, part), f32),
            pltpu.VMEM((waves, 1, 128), i32),
            pltpu.VMEM((members, waves, 1, 128), i32),
            pltpu.VMEM((chunks, waves, members, own_rows * half, part), f32),
            pltpu.VMEM((chunks, fold * total_cells, own_rows // fold * part), f32),
            pltpu.VMEM((chunks, early, own_rows, part), f32),
            pltpu.VMEM((chunks, total_cells, own_rows, part), f32),
            pltpu.VMEM((chunks, groups * owners, own_rows, part), f32),
            dma((3,)),
            dma((4,)),
            dma((chunks, listed_total)),
            pltpu.SemaphoreType.REGULAR,
            pltpu.SemaphoreType.REGULAR,
            dma,
            dma,
            dma((chunks, waves)),
            dma((chunks, waves)),
            dma((chunks,)),
            dma((chunks,)),
        ],
        compiler_params=pltpu.CompilerParams(
            collective_id=0, has_side_effects=True
        ),
    )(
        jnp.transpose(direction, (2, 0, 1)), bin_index, group_index, item_count,
        density, velocity, pressure, normal, weights,
    )


def solution(mesh):
    placed = (
        P(None, ("obs", "face")),
        P(None, None, ("obs", "face")),
        P(None, ("obs", "face")),
        P(None, ("obs", "face")),
        P(("obs", "face"), None, None),
        P(("obs", "face"), None, None, None),
        P(("obs", "face"), None),
        P(("obs", "face"), None),
        P(("obs", "face")),
    )
    return jax.shard_map(
        local, mesh=mesh, in_specs=placed, out_specs=P("face", "obs"), check_vma=False
    )
```

time: 16.6 us -> 15.2 us (0.916)
  Pallas kernels: 15.1 us -> 13.7 us
    pallas_call x1, Pallas kernels: 15.1 us -> 13.7 us  [local(): pl.pallas_call(functools.partial(kernel, n_obs, n_face, planes, cores, ch...]
where the time goes in v3:
time: 15.2 us; the launch traced here: 15 us
  Pallas kernels  13.7 us (90%)
  between operations  0.66 us (4%)
  local copies, waits for them, and re-layouts  0.62 us (4%)
    pallas_call x1, Pallas kernels, local(): pl.pallas_call(functools.partial(kernel, n_obs, n_face, planes, cores, ch...  13.7 us
    unnamed x1, local copies, waits for them, and re-layouts  0.62 us

profile of v3, /device:TPU:0, one launch (start us, length us, event | category | flops | bytes accessed | tf_op | source)
XLA Modules:
  0.0 15.0 jit_solution(2679386611870991581)
XLA Ops:
  0.7 13.7 %shard_map.91 = f32[32,256]{1,0:T(8,128)S(1)} custom-call(f32[3,1,8]{2,1,0:T(1,128)} %bitcast.1, s32[1,8]{1,0:T(1,128)} %bin_in.1, s32[1,8]{1,0:T(1,128)} %group_in.1, s32[1]{0:T(128)S(6)} %copy.12.item_count, f32[34,256]{1,0:T(8,128)} %density.1, f32[3,34,256]{2,1,0:T(8,128)} %velocity.1, f32[34,256]{1,0:T(8,128)} %pressure.1, f32[3,256]{1,0:T(4,128)} %normal.1, ...), custom_call_target="tpu_custom_call" | custom-call | tf_op jit(solution)/shard_map/pallas_call | solution.py:376
  14.4 0.6 %copy.11 = f32[32,256]{1,0:T(8,128)} copy(f32[32,256]{1,0:T(8,128)S(1)} %shard_map.91) | data formatting | bytes 65536

commit v4 on v3

--- a/solution.py
+++ b/solution.py
@@ -10,7 +10,7 @@
 MESH = pl.DeviceIdType.MESH
 BATCH = 8
 SLOT_CAP = 2
-EARLY = 2
+SPLIT = (4, 4, 2)
 PLANES = 1
 
 
@@ -23,7 +23,7 @@
 
 
 def kernel(
-    n_obs, n_face, planes, cores, chunks, early,
+    n_obs, n_face, planes, cores, chunks, sizes,
     direction_in, bin_in, group_in, item_count,
     density, velocity, pressure, normal, weights,
     out,
@@ -42,13 +42,13 @@
     owners = planes * owners_plane
     rows = steps // owners
     total_cells = n_obs * n_face
-    waves, half = products.shape[1], listed_total // products.shape[1]
-    fold = max(1, 8 // half)
-    tile = fold * half
-    tiles = rows // fold
-    lanes = min(128, members * tile)
-    per_row = lanes // tile
-    key_blocks = members // per_row
+    waves = len(sizes)
+    starts = [sum(sizes[:wave]) for wave in range(waves + 1)]
+    ended = [start // SLOT_CAP for start in starts]
+    folds = [max(1, 8 // size) for size in sizes]
+    tiles = [fold * size for fold, size in zip(folds, sizes)]
+    lanes = [min(128, members * tile) for tile in tiles]
+    per_row = [wide // tile for wide, tile in zip(lanes, tiles)]
 
     my_group, my_plane = my_obs // planes, lax.rem(my_obs, planes)
     me = my_plane * n_face + my_face
@@ -111,28 +111,35 @@
     for copy in smalls:
         copy.wait()
     live_count = item_count[0]
-    urgent, label_of = [], []
+    kinds = ended[waves - 1]
+    kind_of = []
     for listed in range(listed_total):
         label = group_index[0, listed] * n_face + bin_index[0, listed]
-        live = listed < live_count
-        urgent.append((live & (label < early)).astype(jnp.int32))
-    urgent_total = sum(urgent)
+        kind_of.append(jnp.where((listed < live_count) & (label < kinds), label, kinds))
+    following = [jnp.int32(0)] * (kinds + 1)
+    for kind in range(1, kinds + 1):
+        following[kind] = following[kind - 1] + sum(
+            (of == kind - 1).astype(jnp.int32) for of in kind_of
+        )
     picked = [jnp.int32(0) for _ in range(listed_total)]
-    ahead = jnp.int32(0)
     for listed in range(listed_total):
-        place = jnp.where(urgent[listed] == 1, ahead, urgent_total + listed - ahead)
-        ahead = ahead + urgent[listed]
+        place = jnp.int32(0)
+        for kind in range(kinds + 1):
+            mine = kind_of[listed] == kind
+            place = jnp.where(mine, following[kind], place)
+            following[kind] = following[kind] + mine.astype(jnp.int32)
         picked = [jnp.where(place == at, listed, old) for at, old in enumerate(picked)]
 
-    lane = lax.broadcasted_iota(jnp.int32, (1, 128), 1) - lax.rem(me, per_row) * tile
+    lane = lax.broadcasted_iota(jnp.int32, (1, 128), 1)
     for wave in range(waves):
+        lane_at = lane - lax.rem(me, per_row[wave]) * tiles[wave]
         row = jnp.zeros((1, 128), jnp.int32)
-        for at in range(half):
-            listed = picked[wave * half + at]
+        for at in range(sizes[wave]):
+            listed = picked[starts[wave] + at]
             label = group_index[0, listed] * n_face + bin_index[0, listed] + 1
             label = jnp.where(listed < live_count, label, 0)
-            for copy_at in range(fold):
-                row = jnp.where(lane == copy_at * half + at, label, row)
+            for copy_at in range(folds[wave]):
+                row = jnp.where(lane_at == copy_at * sizes[wave] + at, label, row)
         labels_out[wave] = row
 
     for copy in loads:
@@ -159,22 +166,26 @@
     for slot in range(listed_total):
         prepare(slot)
 
-    def compute(chunk):
+    def compute(chunk, first_wave, last_wave):
+        slots = [
+            (wave, at) for wave in range(first_wave, last_wave) for at in range(sizes[wave])
+        ]
+        for first in range(0, len(slots), BATCH):
+            batch = slots[first:first + BATCH]
+            results = [
+                jnp.dot(
+                    sources[starts[wave] + at],
+                    matrices[chunk][picked[starts[wave] + at]],
+                    preferred_element_type=jnp.float32,
+                )
+                for wave, at in batch
+            ]
+            for (wave, at), product in zip(batch, results):
+                products[wave][chunk, pl.ds(at, steps, stride=sizes[wave]), :] = product
+
+    def await_weights(chunk):
         for listed in range(listed_total):
             weight_copy(chunk, listed).wait()
-        for first in range(0, listed_total, BATCH):
-            batch = range(first, min(first + BATCH, listed_total))
-            results = [
-                jnp.dot(
-                    sources[slot],
-                    matrices[chunk][picked[slot]],
-                    preferred_element_type=jnp.float32,
-                )
-                for slot in batch
-            ]
-            for slot, product in zip(batch, results):
-                wave, at = divmod(slot, half)
-                products[chunk, wave, pl.ds(at, steps, stride=half), :] = product
 
     def label_copy(owner):
         return pltpu.make_async_remote_copy(
@@ -186,14 +197,14 @@
             device_id_type=MESH,
         )
 
-    def rows_of(owner):
-        size = rows * half
+    def rows_of(wave, owner):
+        size = rows * sizes[wave]
         return pl.ds(pl.multiple_of(owner * size, size), size)
 
     def data_copy(chunk, wave, owner):
         return pltpu.make_async_remote_copy(
-            src_ref=products.at[chunk, wave, rows_of(owner)],
-            dst_ref=arrived.at[chunk, wave, me],
+            src_ref=products[wave].at[chunk, rows_of(wave, owner)],
+            dst_ref=arrived[wave].at[chunk, me],
             send_sem=send_sem.at[chunk, wave],
             recv_sem=recv_sem.at[chunk, wave],
             device_id=owner_device(owner),
@@ -209,21 +220,29 @@
         def _():
             loop(0, owners, lambda shift: copy_of(lax.rem(my_owner + shift, owners)).start())
 
-    compute(0)
+    await_weights(0)
+    compute(0, 0, 1)
     pl.semaphore_wait(barrier, jnp.where(is_owner, owners + groups - 2, owners))
+    send_all(functools.partial(data_copy, 0, 0))
+    send_all(label_copy)
 
     @pl.when(jnp.logical_not(is_owner))
     def _():
         loop(0, owners, lambda owner: tell(entered, owner_device(owner)))
 
-    send_all(label_copy)
-    send_all(functools.partial(data_copy, 0, 0))
+    compute(0, 1, waves)
     for chunk in range(1, chunks):
-        compute(chunk)
+        await_weights(chunk)
+        compute(chunk, 0, 1)
         send_all(functools.partial(data_copy, chunk, 0))
+    if waves > 1:
+        send_all(functools.partial(data_copy, 0, 1))
+    for chunk in range(1, chunks):
+        compute(chunk, 1, waves)
     for wave in range(1, waves):
         for chunk in range(chunks):
-            send_all(functools.partial(data_copy, chunk, wave))
+            if (wave, chunk) != (1, 0):
+                send_all(functools.partial(data_copy, chunk, wave))
 
     def wait_bytes(ref, sem):
         pltpu.make_async_copy(ref, ref, sem).wait()
@@ -260,32 +279,34 @@
         labels_in[me] = labels_out[...]
         for chunk in range(chunks):
             for wave in range(waves):
-                arrived[chunk, wave, me] = products[chunk, wave, rows_of(my_owner)]
+                arrived[wave][chunk, me] = products[wave][chunk, rows_of(wave, my_owner)]
         wait_bytes(labels_in.at[pl.ds(0, members - 1)], label_recv)
-        shape = (fold * total_cells, lanes)
-        line = lax.broadcasted_iota(jnp.int32, shape, 0)
-        place = lax.rem(lax.broadcasted_iota(jnp.int32, shape, 1), tile) // half
         chosen = []
-        for wave in range(waves):
+        for wave, (size, fold, tile) in enumerate(zip(sizes, folds, tiles)):
+            shape = (fold * total_cells, lanes[wave])
+            line = lax.broadcasted_iota(jnp.int32, shape, 0)
+            place = lax.rem(lax.broadcasted_iota(jnp.int32, shape, 1), tile) // size
             parts = []
-            for block in range(key_blocks):
-                keys = jnp.sum(labels_in[block * per_row:(block + 1) * per_row, wave], axis=0)
-                match = keys[:, :lanes] + place * total_cells == line + 1
-                live = keys[:, :lanes] > 0
-                parts.append((match & live).astype(jnp.float32).astype(jnp.bfloat16))
+            for first in range(0, members, per_row[wave]):
+                keys = jnp.sum(labels_in[first:first + per_row[wave], wave], axis=0)
+                keys = keys[:, :lanes[wave]]
+                match = (keys + place * total_cells == line + 1) & (keys > 0)
+                parts.append(match.astype(jnp.float32).astype(jnp.bfloat16))
             chosen.append(jnp.concatenate(parts + parts, axis=1))
 
-        for wave in range(waves):
+        for wave, (fold, tile) in enumerate(zip(folds, tiles)):
+            last = wave == waves - 1
+            begin, end = (0, total_cells) if last else ended[wave:wave + 2]
             for chunk in range(chunks):
                 wait_bytes(
-                    arrived.at[chunk, wave, pl.ds(0, members - 1)], recv_sem.at[chunk, wave]
+                    arrived[wave].at[chunk, pl.ds(0, members - 1)], recv_sem.at[chunk, wave]
                 )
                 values = jnp.concatenate(
                     [
-                        arrived[chunk, wave, :, at * tile:(at + 1) * tile, :].reshape(
+                        arrived[wave][chunk, :, at * tile:(at + 1) * tile, :].reshape(
                             members * tile, part
                         )
-                        for at in range(tiles)
+                        for at in range(rows // fold)
                     ],
                     axis=1,
                 )
@@ -296,25 +317,30 @@
                     jnp.concatenate([high, low], axis=0),
                     preferred_element_type=jnp.float32,
                 )
-                if wave > 0:
-                    sums = sums + partial[chunk]
-                if wave < waves - 1:
-                    partial[chunk] = sums
-                count = total_cells if wave == waves - 1 else early
-                target = cells if wave == waves - 1 else first_cells
-                if wave in (0, waves - 1):
-                    for at in range(rows):
-                        tile_at, line_at = divmod(at, fold)
-                        target[chunk, :, at, :] = sums[
-                            line_at * total_cells:line_at * total_cells + count,
-                            tile_at * part:(tile_at + 1) * part,
-                        ]
+                for at in range(rows):
+                    tile_at, line_at = divmod(at, fold)
+                    found = sums[
+                        line_at * total_cells:(line_at + 1) * total_cells,
+                        tile_at * part:(tile_at + 1) * part,
+                    ]
+                    if wave > 0:
+                        found = found + partial[chunk, at]
+                    if last:
+                        cells[chunk, :, at, :] = found
+                    else:
+                        partial[chunk, at] = found
+                        first_cells[chunk, begin:end, at, :] = found[begin:end]
                 if wave == 0 and chunk == 0 and groups > 1:
                     pl.semaphore_wait(ready, groups - 1)
-                if waves > 1 and wave == 0:
-                    send_cells(first_cells, chunk, 0, early)
-                if wave == waves - 1:
-                    send_cells(cells, chunk, early if waves > 1 else 0, total_cells)
+                if last:
+                    send_cells(cells, chunk, kinds, max(kinds, n_face))
+                else:
+                    send_cells(first_cells, chunk, begin, end)
+        for group in range(1, n_obs):
+            for chunk in range(chunks):
+                send_cells(
+                    cells, chunk, max(kinds, group * n_face), (group + 1) * n_face
+                )
 
     senders = groups * owners
     for chunk in range(chunks):
@@ -336,7 +362,7 @@
         wait_bytes(labels_in.at[pl.ds(0, count)], label_send)
         for chunk in range(chunks):
             for wave in range(waves):
-                wait_bytes(arrived.at[chunk, wave, pl.ds(0, count)], send_sem.at[chunk, wave])
+                wait_bytes(arrived[wave].at[chunk, pl.ds(0, count)], send_sem.at[chunk, wave])
 
     @pl.when(is_owner)
     def _():
@@ -365,16 +391,18 @@
     groups = n_obs // planes
     total_cells = n_obs * n_face
     own_rows = steps // owners
-    waves = 2 if listed_total % 2 == 0 and own_rows % max(1, 16 // listed_total) == 0 else 1
-    half = listed_total // waves
-    fold = max(1, 8 // half)
-    early = min(EARLY, half // SLOT_CAP, n_face)
+    sizes = tuple(listed_total // share for share in SPLIT)
+    usable = all(size % SLOT_CAP == 0 and own_rows % max(1, 8 // size) == 0 for size in sizes if size)
+    if sum(sizes) != listed_total or min(sizes) == 0 or not usable:
+        sizes = (listed_total,)
+    waves = len(sizes)
+    early = max(1, sum(sizes[:-1]) // SLOT_CAP)
     smem = pl.BlockSpec(memory_space=pltpu.SMEM)
     anywhere = pl.BlockSpec(memory_space=pl.ANY)
     f32, i32 = jnp.float32, jnp.int32
     dma = pltpu.SemaphoreType.DMA
     return pl.pallas_call(
-        functools.partial(kernel, n_obs, n_face, planes, cores, chunks, early),
+        functools.partial(kernel, n_obs, n_face, planes, cores, chunks, sizes),
         out_shape=pltpu.VMEM((steps, width), f32),
         in_specs=[anywhere] * 3 + [smem] + [anywhere] * 5,
         out_specs=pl.BlockSpec(memory_space=pltpu.VMEM),
@@ -391,11 +419,11 @@
             pltpu.VMEM((3, steps, faces), f32),
             pltpu.VMEM((3, steps, faces), f32),
             pltpu.VMEM((listed_total, steps, depth), jnp.bfloat16),
-            pltpu.VMEM((chunks, waves, steps * half, part), f32),
+            [pltpu.VMEM((chunks, steps * size, part), f32) for size in sizes],
             pltpu.VMEM((waves, 1, 128), i32),
             pltpu.VMEM((members, waves, 1, 128), i32),
-            pltpu.VMEM((chunks, waves, members, own_rows * half, part), f32),
-            pltpu.VMEM((chunks, fold * total_cells, own_rows // fold * part), f32),
+            [pltpu.VMEM((chunks, members, own_rows * size, part), f32) for size in sizes],
+            pltpu.VMEM((chunks, own_rows, total_cells, part), f32),
             pltpu.VMEM((chunks, early, own_rows, part), f32),
             pltpu.VMEM((chunks, total_cells, own_rows, part), f32),
             pltpu.VMEM((chunks, groups * owners, own_rows, part), f32),

time: 15.2 us -> 14.8 us (0.974)
  the two profiles are of different devices: /device:TPU:0 before, /device:TPU:5 now
where the time goes in v4:
time: 14.8 us; the launch traced here: 14.6 us
  Pallas kernels  13.4 us (91%)
  between operations  0.66 us (4%)
  local copies, waits for them, and re-layouts  0.62 us (4%)
    pallas_call x1, Pallas kernels, local(): pl.pallas_call(functools.partial(kernel, n_obs, n_face, planes, cores, ch...  13.4 us
    unnamed x1, local copies, waits for them, and re-layouts  0.62 us

profile of v4, /device:TPU:5, one launch (start us, length us, event | category | flops | bytes accessed | tf_op | source)
XLA Modules:
  0.0 14.6 jit_solution(10208819007076470006)
XLA Ops:
  0.7 13.4 %shard_map.91 = f32[32,256]{1,0:T(8,128)S(1)} custom-call(f32[3,1,8]{2,1,0:T(1,128)} %bitcast.1, s32[1,8]{1,0:T(1,128)} %bin_in.1, s32[1,8]{1,0:T(1,128)} %group_in.1, s32[1]{0:T(128)S(6)} %copy.12.item_count, f32[34,256]{1,0:T(8,128)} %density.1, f32[3,34,256]{2,1,0:T(8,128)} %velocity.1, f32[34,256]{1,0:T(8,128)} %pressure.1, f32[3,256]{1,0:T(4,128)} %normal.1, ...), custom_call_target="tpu_custom_call" | custom-call | tf_op jit(solution)/shard_map/pallas_call | solution.py:404
  14.0 0.6 %copy.11 = f32[32,256]{1,0:T(8,128)} copy(f32[32,256]{1,0:T(8,128)S(1)} %shard_map.91) | data formatting | bytes 65536

commit v5 on v4

--- a/solution.py
+++ b/solution.py
@@ -231,18 +231,18 @@
         loop(0, owners, lambda owner: tell(entered, owner_device(owner)))
 
     compute(0, 1, waves)
-    for chunk in range(1, chunks):
-        await_weights(chunk)
-        compute(chunk, 0, 1)
-        send_all(functools.partial(data_copy, chunk, 0))
     if waves > 1:
         send_all(functools.partial(data_copy, 0, 1))
     for chunk in range(1, chunks):
-        compute(chunk, 1, waves)
-    for wave in range(1, waves):
+        await_weights(chunk)
+        compute(chunk, 0, min(2, waves))
+        for wave in range(min(2, waves)):
+            send_all(functools.partial(data_copy, chunk, wave))
+    for wave in range(2, waves):
         for chunk in range(chunks):
-            if (wave, chunk) != (1, 0):
-                send_all(functools.partial(data_copy, chunk, wave))
+            if chunk > 0:
+                compute(chunk, wave, wave + 1)
+            send_all(functools.partial(data_copy, chunk, wave))
 
     def wait_bytes(ref, sem):
         pltpu.make_async_copy(ref, ref, sem).wait()
@@ -343,7 +343,8 @@
                 )
 
     senders = groups * owners
-    for chunk in range(chunks):
+
+    def collect(chunk):
         @pl.when(is_owner)
         def _():
             wait_bytes(owned.at[chunk, pl.ds(0, senders - 1)], recv_two.at[chunk])
@@ -364,6 +365,9 @@
             for wave in range(waves):
                 wait_bytes(arrived[wave].at[chunk, pl.ds(0, count)], send_sem.at[chunk, wave])
 
+    for chunk in range(chunks - 1):
+        collect(chunk)
+
     @pl.when(is_owner)
     def _():
         drain(owners - 1)
@@ -373,6 +377,8 @@
     @pl.when(jnp.logical_not(is_owner))
     def _():
         drain(owners)
+
+    collect(chunks - 1)
 
 
 def local(

time: 14.8 us -> 14.8 us (level)
  the two profiles are of different devices: /device:TPU:5 before, /device:TPU:0 now
where the time goes in v5:
time: 14.8 us; the launch traced here: 14.6 us
  Pallas kernels  13.4 us (91%)
  between operations  0.66 us (4%)
  local copies, waits for them, and re-layouts  0.62 us (4%)
    pallas_call x1, Pallas kernels, local(): pl.pallas_call(functools.partial(kernel, n_obs, n_face, planes, cores, ch...  13.4 us
    unnamed x1, local copies, waits for them, and re-layouts  0.62 us

profile of v5, /device:TPU:0, one launch (start us, length us, event | category | flops | bytes accessed | tf_op | source)
XLA Modules:
  0.0 14.6 jit_solution(3571623572699458941)
XLA Ops:
  0.7 13.4 %shard_map.91 = f32[32,256]{1,0:T(8,128)S(1)} custom-call(f32[3,1,8]{2,1,0:T(1,128)} %bitcast.1, s32[1,8]{1,0:T(1,128)} %bin_in.1, s32[1,8]{1,0:T(1,128)} %group_in.1, s32[1]{0:T(128)S(6)} %copy.12.item_count, f32[34,256]{1,0:T(8,128)} %density.1, f32[3,34,256]{2,1,0:T(8,128)} %velocity.1, f32[34,256]{1,0:T(8,128)} %pressure.1, f32[3,256]{1,0:T(4,128)} %normal.1, ...), custom_call_target="tpu_custom_call" | custom-call | tf_op jit(solution)/shard_map/pallas_call | solution.py:410
  14.0 0.6 %copy.11 = f32[32,256]{1,0:T(8,128)} copy(f32[32,256]{1,0:T(8,128)S(1)} %shard_map.91) | data formatting | bytes 65536

commit v6 on v4

--- a/solution.py
+++ b/solution.py
@@ -263,8 +263,13 @@
             def _():
                 cell_copy(source, chunk, cell).start()
 
-        for cell in range(first, last):
-            send(cell)
+        if last <= min(n_face, 8):
+            for core in reversed(range(cores)):
+                for cell in range(first, last):
+                    if cell % cores == core:
+                        send(cell)
+        else:
+            loop(first, last, send)
 
         @pl.when((my_cell >= first) & (my_cell < last))
         def _():
@@ -343,7 +348,8 @@
                 )
 
     senders = groups * owners
-    for chunk in range(chunks):
+
+    def collect(chunk):
         @pl.when(is_owner)
         def _():
             wait_bytes(owned.at[chunk, pl.ds(0, senders - 1)], recv_two.at[chunk])
@@ -364,6 +370,9 @@
             for wave in range(waves):
                 wait_bytes(arrived[wave].at[chunk, pl.ds(0, count)], send_sem.at[chunk, wave])
 
+    for chunk in range(chunks - 1):
+        collect(chunk)
+
     @pl.when(is_owner)
     def _():
         drain(owners - 1)
@@ -373,6 +382,8 @@
     @pl.when(jnp.logical_not(is_owner))
     def _():
         drain(owners)
+
+    collect(chunks - 1)
 
 
 def local(

time: 14.8 us -> 14.7 us (level)
  the two profiles are of different devices: /device:TPU:5 before, /device:TPU:13 now
where the time goes in v6:
time: 14.7 us; the launch traced here: 14.6 us
  Pallas kernels  13.3 us (90%)
  between operations  0.66 us (4%)
  local copies, waits for them, and re-layouts  0.62 us (4%)
    pallas_call x1, Pallas kernels, local(): pl.pallas_call(functools.partial(kernel, n_obs, n_face, planes, cores, ch...  13.3 us
    unnamed x1, local copies, waits for them, and re-layouts  0.62 us

profile of v6, /device:TPU:13, one launch (start us, length us, event | category | flops | bytes accessed | tf_op | source)
XLA Modules:
  0.0 14.6 jit_solution(10521561731512371195)
XLA Ops:
  0.7 13.3 %shard_map.91 = f32[32,256]{1,0:T(8,128)S(1)} custom-call(f32[3,1,8]{2,1,0:T(1,128)} %bitcast.1, s32[1,8]{1,0:T(1,128)} %bin_in.1, s32[1,8]{1,0:T(1,128)} %group_in.1, s32[1]{0:T(128)S(6)} %copy.12.item_count, f32[34,256]{1,0:T(8,128)} %density.1, f32[3,34,256]{2,1,0:T(8,128)} %velocity.1, f32[34,256]{1,0:T(8,128)} %pressure.1, f32[3,256]{1,0:T(4,128)} %normal.1, ...), custom_call_target="tpu_custom_call" | custom-call | tf_op jit(solution)/shard_map/pallas_call | solution.py:415
  13.9 0.6 %copy.11 = f32[32,256]{1,0:T(8,128)} copy(f32[32,256]{1,0:T(8,128)S(1)} %shard_map.91) | data formatting | bytes 65536

commit v7 on v5

--- a/solution.py
+++ b/solution.py
@@ -263,8 +263,13 @@
             def _():
                 cell_copy(source, chunk, cell).start()
 
-        for cell in range(first, last):
-            send(cell)
+        if last <= min(n_face, 8):
+            for core in reversed(range(cores)):
+                for cell in range(first, last):
+                    if cell % cores == core:
+                        send(cell)
+        else:
+            loop(first, last, send)
 
         @pl.when((my_cell >= first) & (my_cell < last))
         def _():

time: 14.8 us -> 14.8 us (level)
  no operation moved by 1% of the time
where the time goes in v7:
time: 14.8 us; the launch traced here: 14.6 us
  Pallas kernels  13.4 us (91%)
  between operations  0.66 us (4%)
  local copies, waits for them, and re-layouts  0.62 us (4%)
    pallas_call x1, Pallas kernels, local(): pl.pallas_call(functools.partial(kernel, n_obs, n_face, planes, cores, ch...  13.4 us
    unnamed x1, local copies, waits for them, and re-layouts  0.62 us

profile of v7, /device:TPU:0, one launch (start us, length us, event | category | flops | bytes accessed | tf_op | source)
XLA Modules:
  0.0 14.6 jit_solution(12805109976454305683)
XLA Ops:
  0.7 13.4 %shard_map.91 = f32[32,256]{1,0:T(8,128)S(1)} custom-call(f32[3,1,8]{2,1,0:T(1,128)} %bitcast.1, s32[1,8]{1,0:T(1,128)} %bin_in.1, s32[1,8]{1,0:T(1,128)} %group_in.1, s32[1]{0:T(128)S(6)} %copy.12.item_count, f32[34,256]{1,0:T(8,128)} %density.1, f32[3,34,256]{2,1,0:T(8,128)} %velocity.1, f32[34,256]{1,0:T(8,128)} %pressure.1, f32[3,256]{1,0:T(4,128)} %normal.1, ...), custom_call_target="tpu_custom_call" | custom-call | tf_op jit(solution)/shard_map/pallas_call | solution.py:415
  14.0 0.6 %copy.11 = f32[32,256]{1,0:T(8,128)} copy(f32[32,256]{1,0:T(8,128)S(1)} %shard_map.91) | data formatting | bytes 65536
